TPU v7x, 512 devices: a whole 4x8x8 slice. The times are simulated.
512 devices in a mesh: gx: 16 (over z, core), gy: 4 (over x), gz: 8 (over y).
Axes of the slice: x: 4, y: 8, z: 8, core: 2. Of those that a mesh axis runs over, the one named last changes fastest.
Arguments:
- krylov_basis: float32 [60, 64, 32, 1024], P(None, 'gx', 'gy', 'gz'), may hold values from -6 to 6
- schur_vectors: float32 [60, 20], replicated, may hold values from -1 to 1, as said below
- next_vector: float32 [64, 32, 1024], P('gx', 'gy', 'gz'), may hold values from -10 to 10
- diag_shift: float32 [64, 32, 1024], P('gx', 'gy', 'gz'), may hold values from 0.25 to 2
- velocity: float32 [3, 64, 32, 1024], P(None, 'gx', 'gy', 'gz'), may hold values from -1 to 1
Outputs:
- new_basis: float32 [24, 64, 32, 1024], P(None, 'gx', 'gy', 'gz')
- hessenberg: float32 [24, 3], replicated
Inputs may be any that keep to these rules, and one draw needn't show every extreme that they name: `schur_vectors`: the columns are orthonormal.
All inputs are finite; a program needn't handle non-finite values.
Results may differ from a plain program's by a relative error of at most 0.0003.
Values sent between devices are 32-bit elements; how exact they have to be, the bound alone decides.
No kernel may reach another device: no remote copies, remote signals or barrier semaphores. Data moves between devices by JAX's collectives and lax.ppermute only.
A program may use at most 64 MiB of HBM per device.

v0:
```python
import jax
import jax.numpy as jnp
from jax import lax
from jax.sharding import Mesh
from jax.sharding import PartitionSpec as P

KEEP = 20
EXPAND = 3
ROWS = 24
GX = ("gx_0", "gx_1")
GX_GY_GZ = ("gx_0", "gx_1", "gy", "gz")


def with_halo(value, sides, width):
    for axis, dim in sides:
        count, length = (lax.axis_size(axis), value.shape[dim])
        up = [(i, (i + 1) % count) for i in range(count - 1)]
        down = [(j, i) for i, j in up]
        last = lax.slice_in_dim(value, length - width, length, axis=dim)
        initial = lax.slice_in_dim(value, 0, width, axis=dim)
        before = lax.ppermute(last, axis, up)
        after = lax.ppermute(initial, axis, down)
        value = jnp.concatenate([before, value, after], axis=dim)
    return value


def by_axis(value, axes):
    for axis in axes:
        value = lax.psum(value, axis)
    return value


def combine_terms(
    field, x_ahead, x_behind, y_ahead, y_behind, z_ahead, z_behind, diag_shift, velocity
):
    neighbours = x_ahead + x_behind + y_ahead + y_behind + z_ahead + z_behind
    flow = (
        velocity[0] * (x_ahead - x_behind)
        + velocity[1] * (y_ahead - y_behind)
        + velocity[2] * (z_ahead - z_behind)
    )
    return (6.0 + diag_shift) * field - neighbours + 0.5 * flow


def operate_field(field, diag_shift, velocity):
    along_x = with_halo(field, ((GX, 0),), 1)
    along_y = with_halo(field, (("gy", 1),), 1)
    along_z = with_halo(field, (("gz", 2),), 1)
    return combine_terms(
        field,
        along_x[2:],
        along_x[:-2],
        along_y[:, 2:],
        along_y[:, :-2],
        along_z[:, :, 2:],
        along_z[:, :, :-2],
        diag_shift,
        velocity,
    )


def per_device(krylov_basis, schur_vectors, next_vector, diag_shift, velocity):
    highest = lax.Precision.HIGHEST
    shape_local = next_vector.shape
    cell_count = (
        shape_local[0]
        * shape_local[1]
        * shape_local[2]
        * lax.axis_size(GX)
        * lax.axis_size("gy")
        * lax.axis_size("gz")
    )
    rotated = jnp.einsum("ik,ixyz->kxyz", schur_vectors, krylov_basis, precision=highest)
    columns = []
    starting = jnp.concatenate([rotated, next_vector[None]], axis=0)
    flat_start = starting.reshape(KEEP + 1, -1)
    gram_matrix = (
        by_axis(jnp.dot(flat_start, flat_start.T, precision=highest), GX_GY_GZ) / cell_count
    )
    divisor = jnp.maximum(jnp.sqrt(gram_matrix[KEEP, KEEP]), 0.5)
    factor = jnp.ones((KEEP + 1,), jnp.float32).at[KEEP].set(1.0 / divisor)
    gram_matrix = gram_matrix * factor[:, None] * factor[None, :]
    vectors = jnp.concatenate([rotated, (next_vector / divisor)[None]], axis=0)
    for expansion in range(EXPAND):
        count = vectors.shape[0]
        flat_basis = vectors.reshape(count, -1)
        applied = operate_field(vectors[-1], diag_shift, velocity).reshape(-1)
        dotted, self_sum = (
            by_axis(jnp.dot(flat_basis, applied, precision=highest), GX_GY_GZ),
            by_axis(jnp.sum(applied * applied), GX_GY_GZ),
        )
        first_coeffs = dotted / cell_count
        self_norm = self_sum / cell_count
        second_coeffs = first_coeffs - jnp.dot(gram_matrix, first_coeffs, precision=highest)
        total_coeffs = first_coeffs + second_coeffs
        partly = applied - jnp.dot(first_coeffs, flat_basis, precision=highest)
        cleaned = partly - jnp.dot(second_coeffs, flat_basis, precision=highest)
        length_sq = (
            self_norm
            - 2.0 * jnp.dot(total_coeffs, first_coeffs, precision=highest)
            + jnp.dot(
                total_coeffs,
                jnp.dot(gram_matrix, total_coeffs, precision=highest),
                precision=highest,
            )
        )
        length = jnp.sqrt(jnp.maximum(length_sq, 0.0))
        divisor = jnp.maximum(length, 0.5)
        column = jnp.zeros((ROWS,), jnp.float32)
        column = column.at[:count].set(total_coeffs).at[count].set(length)
        columns.append(column)
        newest = (cleaned / divisor).reshape(shape_local)
        vectors = jnp.concatenate([vectors, newest[None]], axis=0)
        intersect = (
            second_coeffs - jnp.dot(gram_matrix, second_coeffs, precision=highest)
        ) / divisor
        corner = jnp.maximum(length_sq, 0.0) / (divisor * divisor)
        upper_rows = jnp.concatenate([gram_matrix, intersect[:, None]], axis=1)
        lower_row = jnp.concatenate([intersect, corner[None]], axis=0)
        gram_matrix = jnp.concatenate([upper_rows, lower_row[None]], axis=0)
    return (vectors, jnp.stack(columns, axis=1))


def solution(mesh):
    split = Mesh(
        mesh.devices.reshape(8, 2, mesh.shape["gy"], mesh.shape["gz"]), ("gx_0", "gx_1", "gy", "gz")
    )
    return jax.shard_map(
        per_device,
        mesh=split,
        in_specs=(
            P(None, GX, "gy", "gz"),
            P(),
            P(GX, "gy", "gz"),
            P(GX, "gy", "gz"),
            P(None, GX, "gy", "gz"),
        ),
        out_specs=(P(None, GX, "gy", "gz"), P()),
        check_vma=False,
    )
```

profile of v0, /device:TPU:2, one launch (start us, length us, event | category | flops | bytes accessed | tf_op | source)
XLA Modules:
  0.0 304.2 jit_solution(8931274093424022285)
XLA Ops:
  1.8 1.9 fusion.10
  4.2 35.9 %psum.196 = f32[21,21]{1,0:T(8,128)S(1)} all-reduce(f32[21,21]{1,0:T(8,128)S(1)} %convolution_bitcast_fusion), channel_id=1, replica_groups=mesh['gx_0'=8,'gx_1'=2,'gy'=4,'gz'=8] {'gx_0'}, use_global_device_ids=true, to_apply=%region_0.0 | all-reduce | flops 441 | bytes 3528 | tf_op jit(solution)/shard_map/psum | solution.py:29
  40.2 3.3 %psum.197 = f32[21,21]{1,0:T(8,128)S(1)} all-reduce(f32[21,21]{1,0:T(8,128)S(1)} %psum.196), channel_id=1, replica_groups=mesh['gx_0'=8,'gx_1'=2,'gy'=4,'gz'=8] {'gx_1'}, use_global_device_ids=true, to_apply=%region_1.0 | all-reduce | flops 441 | bytes 3528 | tf_op jit(solution)/shard_map/psum | solution.py:29
  43.4 13.9 %psum.198 = f32[21,21]{1,0:T(8,128)S(1)} all-reduce(f32[21,21]{1,0:T(8,128)S(1)} %psum.197), channel_id=1, replica_groups=mesh['gx_0'=8,'gx_1'=2,'gy'=4,'gz'=8] {'gy'}, use_global_device_ids=true, to_apply=%region_2.0 | all-reduce | flops 441 | bytes 3528 | tf_op jit(solution)/shard_map/psum | solution.py:29
  57.3 30.3 %psum.199 = f32[21,21]{1,0:T(8,128)S(1)} all-reduce(f32[21,21]{1,0:T(8,128)S(1)} %psum.198), channel_id=1, replica_groups=mesh['gx_0'=8,'gx_1'=2,'gy'=4,'gz'=8] {'gz'}, use_global_device_ids=true, to_apply=%region_3.0 | all-reduce | flops 441 | bytes 3528 | tf_op jit(solution)/shard_map/psum | solution.py:29
  89.0 1.5 collective-permute-start.5
  90.6 4.2 %collective-permute-start.3 = (f32[4,1,128]{2,1,0:T(1,128)S(1)}, f32[4,1,128]{2,1,0:T(1,128)S(1)}, u32[]{:S(2)}, u32[]{:S(2)}) collective-permute-start(f32[4,1,128]{2,1,0:T(1,128)S(1)} %get-tuple-element.141), channel_id=1, source_target_pairs={{0,8},{8,16},{16,24},{1,9},{9,17},{17,25},{2,10},{10,18},{18,26},{... | collective-permute-start | bytes 6152 | tf_op jit(solution)/shard_map/ppermute | solution.py:21
  94.8 2.5 collective-permute-start.2
  98.6 1.3 collective-permute-start
  100.3 1.3 collective-permute-start.4
  101.8 4.1 %collective-permute-done.4 = f32[4,8,1]{2,1,0:T(8,128)S(1)} collective-permute-done((f32[4,8,1]{2,1,0:T(8,128)S(1)}, f32[4,8,1]{2,1,0:T(8,128)S(1)}, u32[]{:S(2)}, u32[]{:S(2)}) %collective-permute-start.4) | collective-permute-done | bytes 160 | tf_op jit(solution)/shard_map/ppermute | solution.py:22
  107.1 17.5 %all-reduce.9 = (f32[21]{0:T(128)S(1)}, f32[]{:T(128)}) all-reduce(f32[21]{0:T(128)S(1)} %convolution_bitcast_fusion.11, f32[]{:T(128)} %get-tuple-element.124), channel_id=1, replica_groups=mesh['gx_0'=8,'gx_1'=2,'gy'=4,'gz'=8] {'gx_0'}, use_global_device_ids=true, to_apply=%region_4.0 | all-reduce | flops 22 | bytes 176 | tf_op jit(solution)/shard_map/psum | solution.py:29
  124.6 3.1 %all-reduce.15 = (f32[21]{0:T(128)S(1)}, f32[]{:T(128)}) all-reduce(f32[21]{0:T(128)S(1)} %get-tuple-element.100, f32[]{:T(128)} %get-tuple-element.101), channel_id=1, replica_groups=mesh['gx_0'=8,'gx_1'=2,'gy'=4,'gz'=8] {'gx_1'}, use_global_device_ids=true, to_apply=%region_5.0 | all-reduce | flops 22 | bytes 176 | tf_op jit(solution)/shard_map/psum | solution.py:29
  127.7 9.2 %all-reduce.12 = (f32[21]{0:T(128)S(1)}, f32[]{:T(128)}) all-reduce(f32[21]{0:T(128)S(1)} %get-tuple-element.112, f32[]{:T(128)} %get-tuple-element.113), channel_id=1, replica_groups=mesh['gx_0'=8,'gx_1'=2,'gy'=4,'gz'=8] {'gy'}, use_global_device_ids=true, to_apply=%region_6.0 | all-reduce | flops 22 | bytes 176 | tf_op jit(solution)/shard_map/psum | solution.py:29
  136.9 17.9 %all-reduce.6 = (f32[21]{0:T(128)S(1)}, f32[]{:T(128)}) all-reduce(f32[21]{0:T(128)S(1)} %get-tuple-element.106, f32[]{:T(128)} %get-tuple-element.107), channel_id=1, replica_groups=mesh['gx_0'=8,'gx_1'=2,'gy'=4,'gz'=8] {'gz'}, use_global_device_ids=true, to_apply=%region_7.0 | all-reduce | flops 22 | bytes 176 | tf_op jit(solution)/shard_map/psum | solution.py:29
  159.1 1.6 collective-permute-start.11
  160.8 2.3 collective-permute-start.9
  163.1 3.6 %collective-permute-start.8 = (f32[4,1,128]{2,1,0:T(1,128)S(1)}, f32[4,1,128]{2,1,0:T(1,128)S(1)}, u32[]{:S(2)}, u32[]{:S(2)}) collective-permute-start(f32[4,1,128]{2,1,0:T(1,128)S(1)} %get-tuple-element.134), channel_id=1, source_target_pairs={{8,0},{16,8},{24,16},{9,1},{17,9},{25,17},{10,2},{18,10},{26,18},{... | collective-permute-start | bytes 6152 | tf_op jit(solution)/shard_map/ppermute | solution.py:22
  167.9 1.3 collective-permute-start.6
  170.9 4.5 %collective-permute-done.10 = f32[4,8,1]{2,1,0:T(8,128)S(1)} collective-permute-done((f32[4,8,1]{2,1,0:T(8,128)S(1)}, f32[4,8,1]{2,1,0:T(8,128)S(1)}, u32[]{:S(2)}, u32[]{:S(2)}) %collective-permute-start.10) | collective-permute-done | bytes 160 | tf_op jit(solution)/shard_map/ppermute | solution.py:22
  176.6 19.1 %all-reduce.8 = (f32[22]{0:T(128)S(1)}, f32[]{:T(128)}) all-reduce(f32[22]{0:T(128)S(1)} %convolution_bitcast_fusion.10, f32[]{:T(128)} %get-tuple-element.120), channel_id=1, replica_groups=mesh['gx_0'=8,'gx_1'=2,'gy'=4,'gz'=8] {'gx_0'}, use_global_device_ids=true, to_apply=%region_13.0 | all-reduce | flops 23 | bytes 184 | tf_op jit(solution)/shard_map/psum | solution.py:29
  195.8 3.1 %all-reduce.14 = (f32[22]{0:T(128)S(1)}, f32[]{:T(128)}) all-reduce(f32[22]{0:T(128)S(1)} %get-tuple-element.98, f32[]{:T(128)} %get-tuple-element.99), channel_id=1, replica_groups=mesh['gx_0'=8,'gx_1'=2,'gy'=4,'gz'=8] {'gx_1'}, use_global_device_ids=true, to_apply=%region_14.0 | all-reduce | flops 23 | bytes 184 | tf_op jit(solution)/shard_map/psum | solution.py:29
  198.8 8.1 %all-reduce.11 = (f32[22]{0:T(128)S(1)}, f32[]{:T(128)}) all-reduce(f32[22]{0:T(128)S(1)} %get-tuple-element.110, f32[]{:T(128)} %get-tuple-element.111), channel_id=1, replica_groups=mesh['gx_0'=8,'gx_1'=2,'gy'=4,'gz'=8] {'gy'}, use_global_device_ids=true, to_apply=%region_15.0 | all-reduce | flops 23 | bytes 184 | tf_op jit(solution)/shard_map/psum | solution.py:29
  206.9 19.2 %all-reduce.5 = (f32[22]{0:T(128)S(1)}, f32[]{:T(128)}) all-reduce(f32[22]{0:T(128)S(1)} %get-tuple-element.104, f32[]{:T(128)} %get-tuple-element.105), channel_id=1, replica_groups=mesh['gx_0'=8,'gx_1'=2,'gy'=4,'gz'=8] {'gz'}, use_global_device_ids=true, to_apply=%region_16.0 | all-reduce | flops 23 | bytes 184 | tf_op jit(solution)/shard_map/psum | solution.py:29
  230.6 1.6 collective-permute-start.17
  232.2 3.0 collective-permute-start.15
  235.2 2.9 collective-permute-start.14
  242.4 4.5 %collective-permute-done.16 = f32[4,8,1]{2,1,0:T(8,128)S(1)} collective-permute-done((f32[4,8,1]{2,1,0:T(8,128)S(1)}, f32[4,8,1]{2,1,0:T(8,128)S(1)}, u32[]{:S(2)}, u32[]{:S(2)}) %collective-permute-start.16) | collective-permute-done | bytes 160 | tf_op jit(solution)/shard_map/ppermute | solution.py:22
  248.1 19.0 %all-reduce.7 = (f32[23]{0:T(128)S(1)}, f32[]{:T(128)}) all-reduce(f32[23]{0:T(128)S(1)} %convolution_bitcast_fusion.9, f32[]{:T(128)} %get-tuple-element.116), channel_id=1, replica_groups=mesh['gx_0'=8,'gx_1'=2,'gy'=4,'gz'=8] {'gx_0'}, use_global_device_ids=true, to_apply=%region_22.0 | all-reduce | flops 24 | bytes 192 | tf_op jit(solution)/shard_map/psum | solution.py:29
  267.1 3.1 %all-reduce.13 = (f32[23]{0:T(128)S(1)}, f32[]{:T(128)}) all-reduce(f32[23]{0:T(128)S(1)} %get-tuple-element.96, f32[]{:T(128)} %get-tuple-element.97), channel_id=1, replica_groups=mesh['gx_0'=8,'gx_1'=2,'gy'=4,'gz'=8] {'gx_1'}, use_global_device_ids=true, to_apply=%region_23.0 | all-reduce | flops 24 | bytes 192 | tf_op jit(solution)/shard_map/psum | solution.py:29
  270.2 8.8 %all-reduce.10 = (f32[23]{0:T(128)S(1)}, f32[]{:T(128)}) all-reduce(f32[23]{0:T(128)S(1)} %get-tuple-element.108, f32[]{:T(128)} %get-tuple-element.109), channel_id=1, replica_groups=mesh['gx_0'=8,'gx_1'=2,'gy'=4,'gz'=8] {'gy'}, use_global_device_ids=true, to_apply=%region_24.0 | all-reduce | flops 24 | bytes 192 | tf_op jit(solution)/shard_map/psum | solution.py:29
  278.9 19.2 %all-reduce.4 = (f32[23]{0:T(128)S(1)}, f32[]{:T(128)}) all-reduce(f32[23]{0:T(128)S(1)} %get-tuple-element.102, f32[]{:T(128)} %get-tuple-element.103), channel_id=1, replica_groups=mesh['gx_0'=8,'gx_1'=2,'gy'=4,'gz'=8] {'gz'}, use_global_device_ids=true, to_apply=%region_25.0 | all-reduce | flops 24 | bytes 192 | tf_op jit(solution)/shard_map/psum | solution.py:29
  (85 shorter events, 23.8 us)
Async XLA Ops:
  0.6 1.2 copy-start
  0.6 3.1 %copy-start.3 = (f32[4,8,128]{2,1,0:T(8,128)S(1)}, f32[4,8,128]{2,1,0:T(8,128)}, u32[]{:S(2)}) copy-start(f32[4,8,128]{2,1,0:T(8,128)} %param.21) | copy-start | bytes 49156
  89.0 11.2 %collective-permute-start.5 = (f32[4,8,1]{2,1,0:T(8,128)S(1)}, f32[4,8,1]{2,1,0:T(8,128)S(1)}, u32[]{:S(2)}, u32[]{:S(2)}) collective-permute-start(f32[4,8,1]{2,1,0:T(8,128)S(1)} %get-tuple-element.143), channel_id=1, source_target_pairs={{0,1},{1,2},{2,3},{3,4},{4,5},{5,6},{6,7},{8,9},{9,10},{10,11},{11... | collective-permute-start | bytes 392 | tf_op jit(solution)/shard_map/ppermute | solution.py:21
  90.6 15.3 %collective-permute-start.3 = (f32[4,1,128]{2,1,0:T(1,128)S(1)}, f32[4,1,128]{2,1,0:T(1,128)S(1)}, u32[]{:S(2)}, u32[]{:S(2)}) collective-permute-start(f32[4,1,128]{2,1,0:T(1,128)S(1)} %get-tuple-element.141), channel_id=1, source_target_pairs={{0,8},{8,16},{16,24},{1,9},{9,17},{17,25},{2,10},{10,18},{18,26},{... | collective-permute-start | bytes 6152 | tf_op jit(solution)/shard_map/ppermute | solution.py:21
  94.8 11.2 %collective-permute-start.2 = (f32[4,1,128]{2,1,0:T(1,128)S(1)}, f32[4,1,128]{2,1,0:T(1,128)S(1)}, u32[]{:S(2)}, u32[]{:S(2)}) collective-permute-start(f32[4,1,128]{2,1,0:T(1,128)S(1)} %get-tuple-element.140), channel_id=1, source_target_pairs={{8,0},{16,8},{24,16},{9,1},{17,9},{25,17},{10,2},{18,10},{26,18},{... | collective-permute-start | bytes 6152 | tf_op jit(solution)/shard_map/ppermute | solution.py:22
  97.3 8.6 %collective-permute-start.1 = (f32[1,8,128]{2,1,0:T(8,128)S(1)}, f32[1,8,128]{2,1,0:T(8,128)S(1)}, u32[]{:S(2)}, u32[]{:S(2)}) collective-permute-start(f32[1,8,128]{2,1,0:T(8,128)S(1)} %get-tuple-element.139), channel_id=1, source_target_pairs={{0,32},{32,64},{64,96},{96,128},{128,160},{160,192},{192,224},{224... | collective-permute-start | bytes 12296 | tf_op jit(solution)/shard_map/ppermute | solution.py:21
  98.6 7.4 %collective-permute-start = (f32[1,8,128]{2,1,0:T(8,128)S(1)}, f32[1,8,128]{2,1,0:T(8,128)S(1)}, u32[]{:S(2)}, u32[]{:S(2)}) collective-permute-start(f32[1,8,128]{2,1,0:T(8,128)S(1)} %get-tuple-element.138), channel_id=1, source_target_pairs={{32,0},{64,32},{96,64},{128,96},{160,128},{192,160},{224,192},{256... | collective-permute-start | bytes 12296 | tf_op jit(solution)/shard_map/ppermute | solution.py:22
  100.3 5.6 %collective-permute-start.4 = (f32[4,8,1]{2,1,0:T(8,128)S(1)}, f32[4,8,1]{2,1,0:T(8,128)S(1)}, u32[]{:S(2)}, u32[]{:S(2)}) collective-permute-start(f32[4,8,1]{2,1,0:T(8,128)S(1)} %get-tuple-element.142), channel_id=1, source_target_pairs={{1,0},{2,1},{3,2},{4,3},{5,4},{6,5},{7,6},{9,8},{10,9},{11,10},{12... | collective-permute-start | bytes 392 | tf_op jit(solution)/shard_map/ppermute | solution.py:22
  101.6 4.4 %copy-start.1 = (f32[3,4,8,128]{3,2,1,0:T(8,128)S(1)}, f32[3,4,8,128]{3,2,1,0:T(8,128)}, u32[]{:S(2)}) copy-start(f32[3,4,8,128]{3,2,1,0:T(8,128)} %param.23) | copy-start | bytes 147460
  101.6 4.4 %copy-start.2 = (f32[4,8,128]{2,1,0:T(8,128)S(1)}, f32[4,8,128]{2,1,0:T(8,128)}, u32[]{:S(2)}) copy-start(f32[4,8,128]{2,1,0:T(8,128)} %param.22) | copy-start | bytes 49156
  159.1 10.4 %collective-permute-start.11 = (f32[4,8,1]{2,1,0:T(8,128)S(1)}, f32[4,8,1]{2,1,0:T(8,128)S(1)}, u32[]{:S(2)}, u32[]{:S(2)}) collective-permute-start(f32[4,8,1]{2,1,0:T(8,128)S(1)} %get-tuple-element.137), channel_id=1, source_target_pairs={{0,1},{1,2},{2,3},{3,4},{4,5},{5,6},{6,7},{8,9},{9,10},{10,11},{11... | collective-permute-start | bytes 392 | tf_op jit(solution)/shard_map/ppermute | solution.py:21
  160.8 14.7 %collective-permute-start.9 = (f32[4,1,128]{2,1,0:T(1,128)S(1)}, f32[4,1,128]{2,1,0:T(1,128)S(1)}, u32[]{:S(2)}, u32[]{:S(2)}) collective-permute-start(f32[4,1,128]{2,1,0:T(1,128)S(1)} %get-tuple-element.135), channel_id=1, source_target_pairs={{0,8},{8,16},{16,24},{1,9},{9,17},{17,25},{2,10},{10,18},{18,26},{... | collective-permute-start | bytes 6152 | tf_op jit(solution)/shard_map/ppermute | solution.py:21
  163.1 12.4 %collective-permute-start.8 = (f32[4,1,128]{2,1,0:T(1,128)S(1)}, f32[4,1,128]{2,1,0:T(1,128)S(1)}, u32[]{:S(2)}, u32[]{:S(2)}) collective-permute-start(f32[4,1,128]{2,1,0:T(1,128)S(1)} %get-tuple-element.134), channel_id=1, source_target_pairs={{8,0},{16,8},{24,16},{9,1},{17,9},{25,17},{10,2},{18,10},{26,18},{... | collective-permute-start | bytes 6152 | tf_op jit(solution)/shard_map/ppermute | solution.py:22
  166.6 8.8 %collective-permute-start.7 = (f32[1,8,128]{2,1,0:T(8,128)S(1)}, f32[1,8,128]{2,1,0:T(8,128)S(1)}, u32[]{:S(2)}, u32[]{:S(2)}) collective-permute-start(f32[1,8,128]{2,1,0:T(8,128)S(1)} %get-tuple-element.133), channel_id=1, source_target_pairs={{0,32},{32,64},{64,96},{96,128},{128,160},{160,192},{192,224},{224... | collective-permute-start | bytes 12296 | tf_op jit(solution)/shard_map/ppermute | solution.py:21
  167.9 7.5 %collective-permute-start.6 = (f32[1,8,128]{2,1,0:T(8,128)S(1)}, f32[1,8,128]{2,1,0:T(8,128)S(1)}, u32[]{:S(2)}, u32[]{:S(2)}) collective-permute-start(f32[1,8,128]{2,1,0:T(8,128)S(1)} %get-tuple-element.132), channel_id=1, source_target_pairs={{32,0},{64,32},{96,64},{128,96},{160,128},{192,160},{224,192},{256... | collective-permute-start | bytes 12296 | tf_op jit(solution)/shard_map/ppermute | solution.py:22
  169.5 5.9 %collective-permute-start.10 = (f32[4,8,1]{2,1,0:T(8,128)S(1)}, f32[4,8,1]{2,1,0:T(8,128)S(1)}, u32[]{:S(2)}, u32[]{:S(2)}) collective-permute-start(f32[4,8,1]{2,1,0:T(8,128)S(1)} %get-tuple-element.136), channel_id=1, source_target_pairs={{1,0},{2,1},{3,2},{4,3},{5,4},{6,5},{7,6},{9,8},{10,9},{11,10},{12... | collective-permute-start | bytes 392 | tf_op jit(solution)/shard_map/ppermute | solution.py:22
  230.6 10.4 %collective-permute-start.17 = (f32[4,8,1]{2,1,0:T(8,128)S(1)}, f32[4,8,1]{2,1,0:T(8,128)S(1)}, u32[]{:S(2)}, u32[]{:S(2)}) collective-permute-start(f32[4,8,1]{2,1,0:T(8,128)S(1)} %get-tuple-element.131), channel_id=1, source_target_pairs={{0,1},{1,2},{2,3},{3,4},{4,5},{5,6},{6,7},{8,9},{9,10},{10,11},{11... | collective-permute-start | bytes 392 | tf_op jit(solution)/shard_map/ppermute | solution.py:21
  232.2 14.7 %collective-permute-start.15 = (f32[4,1,128]{2,1,0:T(1,128)S(1)}, f32[4,1,128]{2,1,0:T(1,128)S(1)}, u32[]{:S(2)}, u32[]{:S(2)}) collective-permute-start(f32[4,1,128]{2,1,0:T(1,128)S(1)} %get-tuple-element.129), channel_id=1, source_target_pairs={{0,8},{8,16},{16,24},{1,9},{9,17},{17,25},{2,10},{10,18},{18,26},{... | collective-permute-start | bytes 6152 | tf_op jit(solution)/shard_map/ppermute | solution.py:21
  235.2 11.7 %collective-permute-start.14 = (f32[4,1,128]{2,1,0:T(1,128)S(1)}, f32[4,1,128]{2,1,0:T(1,128)S(1)}, u32[]{:S(2)}, u32[]{:S(2)}) collective-permute-start(f32[4,1,128]{2,1,0:T(1,128)S(1)} %get-tuple-element.128), channel_id=1, source_target_pairs={{8,0},{16,8},{24,16},{9,1},{17,9},{25,17},{10,2},{18,10},{26,18},{... | collective-permute-start | bytes 6152 | tf_op jit(solution)/shard_map/ppermute | solution.py:22
  238.1 8.8 %collective-permute-start.13 = (f32[1,8,128]{2,1,0:T(8,128)S(1)}, f32[1,8,128]{2,1,0:T(8,128)S(1)}, u32[]{:S(2)}, u32[]{:S(2)}) collective-permute-start(f32[1,8,128]{2,1,0:T(8,128)S(1)} %get-tuple-element.127), channel_id=1, source_target_pairs={{0,32},{32,64},{64,96},{96,128},{128,160},{160,192},{192,224},{224... | collective-permute-start | bytes 12296 | tf_op jit(solution)/shard_map/ppermute | solution.py:21
  239.4 7.5 %collective-permute-start.12 = (f32[1,8,128]{2,1,0:T(8,128)S(1)}, f32[1,8,128]{2,1,0:T(8,128)S(1)}, u32[]{:S(2)}, u32[]{:S(2)}) collective-permute-start(f32[1,8,128]{2,1,0:T(8,128)S(1)} %get-tuple-element.126), channel_id=1, source_target_pairs={{32,0},{64,32},{96,64},{128,96},{160,128},{192,160},{224,192},{256... | collective-permute-start | bytes 12296 | tf_op jit(solution)/shard_map/ppermute | solution.py:22
  241.0 5.9 %collective-permute-start.16 = (f32[4,8,1]{2,1,0:T(8,128)S(1)}, f32[4,8,1]{2,1,0:T(8,128)S(1)}, u32[]{:S(2)}, u32[]{:S(2)}) collective-permute-start(f32[4,8,1]{2,1,0:T(8,128)S(1)} %get-tuple-element.130), channel_id=1, source_target_pairs={{1,0},{2,1},{3,2},{4,3},{5,4},{6,5},{7,6},{9,8},{10,9},{11,10},{12... | collective-permute-start | bytes 392 | tf_op jit(solution)/shard_map/ppermute | solution.py:22
where the time goes:
time: 305 us; the launch traced here: 304 us
  blocking collectives  231 us (76%)
  starting transfers between devices  34.8 us (11%)
  waiting for transfers between devices  13.1 us (4%)
  matrix products  10.7 us (4%)
  between operations  7.85 us (3%)
  local copies, waits for them, and re-layouts  4 us (1%)
  other arithmetic  3.16 us (1%)
    psum x16, blocking collectives, by_axis(): value = lax.psum(value, axis)  231 us
    ppermute x9, starting transfers between devices, with_halo(): before = lax.ppermute(last, axis, up)  18.1 us
    ppermute x9, starting transfers between devices, with_halo(): after = lax.ppermute(initial, axis, down)  16.7 us
    ppermute x9, waiting for transfers between devices, with_halo(): after = lax.ppermute(initial, axis, down)  13.1 us
  transfers between devices with their start and end apart: 18, of which 3 were waited for; matrix products, arithmetic and copies ran while one was open for 0% of the time, Pallas kernels for 0%

commit v1 on v0

--- a/solution.py
+++ b/solution.py
@@ -26,7 +26,7 @@
 
 def by_axis(value, axes):
     for axis in axes:
-        value = lax.psum(value, axis)
+        value = jnp.sum(lax.all_gather(value, axis), axis=0)
     return value
 
 

time: 305 us -> 329 us (1.079)
  the two profiles are of different devices: /device:TPU:2 before, /device:TPU:32 now
where the time goes in v1:
time: 329 us; the launch traced here: 327 us
  blocking collectives  218 us (66%)
  starting transfers between devices  39.5 us (12%)
  local copies, waits for them, and re-layouts  29.4 us (9%)
  between operations  15.4 us (5%)
  matrix products  10.8 us (3%)
  other arithmetic  10.7 us (3%)
  waiting for transfers between devices  3.82 us (1%)
    unnamed x12, blocking collectives  148 us
    all_gather x4, blocking collectives, by_axis(): value = jnp.sum(lax.all_gather(value, axis), axis=0)  69.6 us
    unnamed x63, local copies, waits for them, and re-layouts  26.7 us
    ppermute x9, starting transfers between devices, with_halo(): after = lax.ppermute(initial, axis, down)  23.2 us
    ppermute x9, starting transfers between devices, with_halo(): before = lax.ppermute(last, axis, up)  16.4 us
    reduce_sum x28, other arithmetic, by_axis(): value = jnp.sum(lax.all_gather(value, axis), axis=0)  7.56 us
  transfers between devices with their start and end apart: 18, of which 3 were waited for; matrix products, arithmetic and copies ran while one was open for 2% of the time, Pallas kernels for 0%

profile of v1, /device:TPU:32, one launch (start us, length us, event | category | flops | bytes accessed | tf_op | source)
XLA Modules:
  0.0 327.3 jit_solution(13426313026371231723)
XLA Ops:
  1.8 1.9 fusion.10
  4.2 31.0 %all-gather.16 = f32[8,21,21]{2,1,0:T(8,128)S(1)} all-gather(f32[1,21,21]{2,1,0:T(8,128)S(1)} %convolution_bitcast_fusion), channel_id=2, replica_groups=mesh['gx_0'=8,'gx_1'=2,'gy'=4,'gz'=8] {'gx_0'}, dimensions={0}, use_global_device_ids=true | all-gather | bytes 15876 | tf_op jit(solution)/shard_map/all_gather | solution.py:29
  35.2 1.8 all-gather.17
  37.0 12.3 %all-gather.18 = f32[4,21,21]{2,1,0:T(8,128)S(1)} all-gather(f32[1,21,21]{2,1,0:T(8,128)S(1)} %bitcast.333), channel_id=4, replica_groups=mesh['gx_0'=8,'gx_1'=2,'gy'=4,'gz'=8] {'gy'}, dimensions={0}, use_global_device_ids=true | all-gather | bytes 8820 | tf_op jit(solution)/shard_map/all_gather | solution.py:29
  49.3 24.6 %all-gather.19 = f32[8,21,21]{2,1,0:T(8,128)S(1)} all-gather(f32[1,21,21]{2,1,0:T(8,128)S(1)} %bitcast.332), channel_id=5, replica_groups=mesh['gx_0'=8,'gx_1'=2,'gy'=4,'gz'=8] {'gz'}, dimensions={0}, use_global_device_ids=true | all-gather | bytes 15876 | tf_op jit(solution)/shard_map/all_gather | solution.py:29
  75.3 1.9 collective-permute-start.5
  77.2 3.1 collective-permute-start.3
  97.4 5.1 %collective-permute-start.4 = (f32[4,8,1]{2,1,0:T(8,128)S(1)}, f32[4,8,1]{2,1,0:T(8,128)S(1)}, u32[]{:S(2)}, u32[]{:S(2)}) collective-permute-start(f32[4,8,1]{2,1,0:T(8,128)S(1)} %get-tuple-element.146), channel_id=1, source_target_pairs={{1,0},{2,1},{3,2},{4,3},{5,4},{6,5},{7,6},{9,8},{10,9},{11,10},{12... | collective-permute-start | bytes 392 | tf_op jit(solution)/shard_map/ppermute | solution.py:22
  105.4 1.4 dynamic-update-slice.21
  106.8 19.8 %all-reduce.33 = (f32[168]{0:T(256)S(1)}, f32[8]{0:T(128)S(1)}) all-reduce(f32[168]{0:T(256)S(1)} %dynamic-update-slice.17, f32[8]{0:T(128)S(1)} %dynamic-update-slice.21), channel_id=6, replica_groups=mesh['gx_0'=8,'gx_1'=2,'gy'=4,'gz'=8] {'gx_0'}, use_global_device_ids=true, to_apply=%add.4 | all-reduce | flops 176 | bytes 1408
  127.5 1.4 dynamic-update-slice.22
  128.9 2.4 all-reduce.39
  133.6 11.6 %all-reduce.36 = (f32[84]{0:T(128)S(1)}, f32[4]{0:T(128)S(1)}) all-reduce(f32[84]{0:T(128)S(1)} %dynamic-update-slice.19, f32[4]{0:T(128)S(1)} %dynamic-update-slice.23), channel_id=8, replica_groups=mesh['gx_0'=8,'gx_1'=2,'gy'=4,'gz'=8] {'gy'}, use_global_device_ids=true, to_apply=%add.6 | all-reduce | flops 88 | bytes 704
  146.1 1.4 dynamic-update-slice.24
  147.4 17.6 %all-reduce.30 = (f32[168]{0:T(256)S(1)}, f32[8]{0:T(128)S(1)}) all-reduce(f32[168]{0:T(256)S(1)} %dynamic-update-slice.20, f32[8]{0:T(128)S(1)} %dynamic-update-slice.24), channel_id=9, replica_groups=mesh['gx_0'=8,'gx_1'=2,'gy'=4,'gz'=8] {'gz'}, use_global_device_ids=true, to_apply=%add.7 | all-reduce | flops 176 | bytes 1408
  170.2 1.9 collective-permute-start.11
  177.6 5.1 %collective-permute-start.10 = (f32[4,8,1]{2,1,0:T(8,128)S(1)}, f32[4,8,1]{2,1,0:T(8,128)S(1)}, u32[]{:S(2)}, u32[]{:S(2)}) collective-permute-start(f32[4,8,1]{2,1,0:T(8,128)S(1)} %get-tuple-element.140), channel_id=1, source_target_pairs={{1,0},{2,1},{3,2},{4,3},{5,4},{6,5},{7,6},{9,8},{10,9},{11,10},{12... | collective-permute-start | bytes 392 | tf_op jit(solution)/shard_map/ppermute | solution.py:22
  185.4 1.4 dynamic-update-slice.29
  187.0 16.9 %all-reduce.32 = (f32[176]{0:T(256)S(1)}, f32[8]{0:T(128)S(1)}) all-reduce(f32[176]{0:T(256)S(1)} %dynamic-update-slice.25, f32[8]{0:T(128)S(1)} %dynamic-update-slice.29), channel_id=10, replica_groups=mesh['gx_0'=8,'gx_1'=2,'gy'=4,'gz'=8] {'gx_0'}, use_global_device_ids=true, to_apply=%add.12 | all-reduce | flops 184 | bytes 1472
  204.6 1.4 dynamic-update-slice.30
  206.2 2.4 all-reduce.38
  210.9 10.7 %all-reduce.35 = (f32[88]{0:T(128)S(1)}, f32[4]{0:T(128)S(1)}) all-reduce(f32[88]{0:T(128)S(1)} %dynamic-update-slice.27, f32[4]{0:T(128)S(1)} %dynamic-update-slice.31), channel_id=12, replica_groups=mesh['gx_0'=8,'gx_1'=2,'gy'=4,'gz'=8] {'gy'}, use_global_device_ids=true, to_apply=%add.14 | all-reduce | flops 92 | bytes 736
  223.9 17.6 %all-reduce.29 = (f32[176]{0:T(256)S(1)}, f32[8]{0:T(128)S(1)}) all-reduce(f32[176]{0:T(256)S(1)} %dynamic-update-slice.28, f32[8]{0:T(128)S(1)} %dynamic-update-slice.32), channel_id=13, replica_groups=mesh['gx_0'=8,'gx_1'=2,'gy'=4,'gz'=8] {'gz'}, use_global_device_ids=true, to_apply=%add.15 | all-reduce | flops 184 | bytes 1472
  246.6 1.9 collective-permute-start.17
  248.5 2.4 collective-permute-start.15
  255.1 5.1 %collective-permute-start.16 = (f32[4,8,1]{2,1,0:T(8,128)S(1)}, f32[4,8,1]{2,1,0:T(8,128)S(1)}, u32[]{:S(2)}, u32[]{:S(2)}) collective-permute-start(f32[4,8,1]{2,1,0:T(8,128)S(1)} %get-tuple-element.134), channel_id=1, source_target_pairs={{1,0},{2,1},{3,2},{4,3},{5,4},{6,5},{7,6},{9,8},{10,9},{11,10},{12... | collective-permute-start | bytes 392 | tf_op jit(solution)/shard_map/ppermute | solution.py:22
  262.9 1.5 dynamic-update-slice.37
  264.6 18.5 %all-reduce.31 = (f32[184]{0:T(256)S(1)}, f32[8]{0:T(128)S(1)}) all-reduce(f32[184]{0:T(256)S(1)} %dynamic-update-slice.33, f32[8]{0:T(128)S(1)} %dynamic-update-slice.37), channel_id=14, replica_groups=mesh['gx_0'=8,'gx_1'=2,'gy'=4,'gz'=8] {'gx_0'}, use_global_device_ids=true, to_apply=%add.20 | all-reduce | flops 192 | bytes 1536
  283.8 1.4 dynamic-update-slice.38
  285.5 2.4 all-reduce.37
  290.2 10.3 %all-reduce.34 = (f32[92]{0:T(128)S(1)}, f32[4]{0:T(128)S(1)}) all-reduce(f32[92]{0:T(128)S(1)} %dynamic-update-slice.35, f32[4]{0:T(128)S(1)} %dynamic-update-slice.39), channel_id=16, replica_groups=mesh['gx_0'=8,'gx_1'=2,'gy'=4,'gz'=8] {'gy'}, use_global_device_ids=true, to_apply=%add.22 | all-reduce | flops 96 | bytes 768
  302.8 17.6 %all-reduce.28 = (f32[184]{0:T(256)S(1)}, f32[8]{0:T(128)S(1)}) all-reduce(f32[184]{0:T(256)S(1)} %dynamic-update-slice.36, f32[8]{0:T(128)S(1)} %dynamic-update-slice.40), channel_id=17, replica_groups=mesh['gx_0'=8,'gx_1'=2,'gy'=4,'gz'=8] {'gz'}, use_global_device_ids=true, to_apply=%add.23 | all-reduce | flops 192 | bytes 1536
  (177 shorter events, 55.7 us)
Async XLA Ops:
  0.6 1.2 copy-start
  0.6 3.1 copy-start.3
  75.3 22.1 %collective-permute-start.5 = (f32[4,8,1]{2,1,0:T(8,128)S(1)}, f32[4,8,1]{2,1,0:T(8,128)S(1)}, u32[]{:S(2)}, u32[]{:S(2)}) collective-permute-start(f32[4,8,1]{2,1,0:T(8,128)S(1)} %get-tuple-element.147), channel_id=1, source_target_pairs={{0,1},{1,2},{2,3},{3,4},{4,5},{5,6},{6,7},{8,9},{9,10},{10,11},{11... | collective-permute-start | bytes 392 | tf_op jit(solution)/shard_map/ppermute | solution.py:21
  77.2 26.8 %collective-permute-start.3 = (f32[4,1,128]{2,1,0:T(1,128)S(1)}, f32[4,1,128]{2,1,0:T(1,128)S(1)}, u32[]{:S(2)}, u32[]{:S(2)}) collective-permute-start(f32[4,1,128]{2,1,0:T(1,128)S(1)} %get-tuple-element.145), channel_id=1, source_target_pairs={{0,8},{8,16},{16,24},{1,9},{9,17},{17,25},{2,10},{10,18},{18,26},{... | collective-permute-start | bytes 6152 | tf_op jit(solution)/shard_map/ppermute | solution.py:21
  80.3 23.6 %collective-permute-start.2 = (f32[4,1,128]{2,1,0:T(1,128)S(1)}, f32[4,1,128]{2,1,0:T(1,128)S(1)}, u32[]{:S(2)}, u32[]{:S(2)}) collective-permute-start(f32[4,1,128]{2,1,0:T(1,128)S(1)} %get-tuple-element.144), channel_id=1, source_target_pairs={{8,0},{16,8},{24,16},{9,1},{17,9},{25,17},{10,2},{18,10},{26,18},{... | collective-permute-start | bytes 6152 | tf_op jit(solution)/shard_map/ppermute | solution.py:22
  81.6 22.3 %collective-permute-start.1 = (f32[1,8,128]{2,1,0:T(8,128)S(1)}, f32[1,8,128]{2,1,0:T(8,128)S(1)}, u32[]{:S(2)}, u32[]{:S(2)}) collective-permute-start(f32[1,8,128]{2,1,0:T(8,128)S(1)} %get-tuple-element.143), channel_id=1, source_target_pairs={{0,32},{32,64},{64,96},{96,128},{128,160},{160,192},{192,224},{224... | collective-permute-start | bytes 12296 | tf_op jit(solution)/shard_map/ppermute | solution.py:21
  82.9 21.0 %collective-permute-start = (f32[1,8,128]{2,1,0:T(8,128)S(1)}, f32[1,8,128]{2,1,0:T(8,128)S(1)}, u32[]{:S(2)}, u32[]{:S(2)}) collective-permute-start(f32[1,8,128]{2,1,0:T(8,128)S(1)} %get-tuple-element.142), channel_id=1, source_target_pairs={{32,0},{64,32},{96,64},{128,96},{160,128},{192,160},{224,192},{256... | collective-permute-start | bytes 12296 | tf_op jit(solution)/shard_map/ppermute | solution.py:22
  97.4 6.6 %collective-permute-start.4 = (f32[4,8,1]{2,1,0:T(8,128)S(1)}, f32[4,8,1]{2,1,0:T(8,128)S(1)}, u32[]{:S(2)}, u32[]{:S(2)}) collective-permute-start(f32[4,8,1]{2,1,0:T(8,128)S(1)} %get-tuple-element.146), channel_id=1, source_target_pairs={{1,0},{2,1},{3,2},{4,3},{5,4},{6,5},{7,6},{9,8},{10,9},{11,10},{12... | collective-permute-start | bytes 392 | tf_op jit(solution)/shard_map/ppermute | solution.py:22
  102.6 1.4 copy-start.1
  102.6 1.4 copy-start.2
  170.2 7.4 %collective-permute-start.11 = (f32[4,8,1]{2,1,0:T(8,128)S(1)}, f32[4,8,1]{2,1,0:T(8,128)S(1)}, u32[]{:S(2)}, u32[]{:S(2)}) collective-permute-start(f32[4,8,1]{2,1,0:T(8,128)S(1)} %get-tuple-element.141), channel_id=1, source_target_pairs={{0,1},{1,2},{2,3},{3,4},{4,5},{5,6},{6,7},{8,9},{9,10},{10,11},{11... | collective-permute-start | bytes 392 | tf_op jit(solution)/shard_map/ppermute | solution.py:21
  172.1 12.1 %collective-permute-start.9 = (f32[4,1,128]{2,1,0:T(1,128)S(1)}, f32[4,1,128]{2,1,0:T(1,128)S(1)}, u32[]{:S(2)}, u32[]{:S(2)}) collective-permute-start(f32[4,1,128]{2,1,0:T(1,128)S(1)} %get-tuple-element.139), channel_id=1, source_target_pairs={{0,8},{8,16},{16,24},{1,9},{9,17},{17,25},{2,10},{10,18},{18,26},{... | collective-permute-start | bytes 6152 | tf_op jit(solution)/shard_map/ppermute | solution.py:21
  173.4 10.8 %collective-permute-start.8 = (f32[4,1,128]{2,1,0:T(1,128)S(1)}, f32[4,1,128]{2,1,0:T(1,128)S(1)}, u32[]{:S(2)}, u32[]{:S(2)}) collective-permute-start(f32[4,1,128]{2,1,0:T(1,128)S(1)} %get-tuple-element.138), channel_id=1, source_target_pairs={{8,0},{16,8},{24,16},{9,1},{17,9},{25,17},{10,2},{18,10},{26,18},{... | collective-permute-start | bytes 6152 | tf_op jit(solution)/shard_map/ppermute | solution.py:22
  174.7 9.5 %collective-permute-start.7 = (f32[1,8,128]{2,1,0:T(8,128)S(1)}, f32[1,8,128]{2,1,0:T(8,128)S(1)}, u32[]{:S(2)}, u32[]{:S(2)}) collective-permute-start(f32[1,8,128]{2,1,0:T(8,128)S(1)} %get-tuple-element.137), channel_id=1, source_target_pairs={{0,32},{32,64},{64,96},{96,128},{128,160},{160,192},{192,224},{224... | collective-permute-start | bytes 12296 | tf_op jit(solution)/shard_map/ppermute | solution.py:21
  176.0 8.2 %collective-permute-start.6 = (f32[1,8,128]{2,1,0:T(8,128)S(1)}, f32[1,8,128]{2,1,0:T(8,128)S(1)}, u32[]{:S(2)}, u32[]{:S(2)}) collective-permute-start(f32[1,8,128]{2,1,0:T(8,128)S(1)} %get-tuple-element.136), channel_id=1, source_target_pairs={{32,0},{64,32},{96,64},{128,96},{160,128},{192,160},{224,192},{256... | collective-permute-start | bytes 12296 | tf_op jit(solution)/shard_map/ppermute | solution.py:22
  177.6 6.6 %collective-permute-start.10 = (f32[4,8,1]{2,1,0:T(8,128)S(1)}, f32[4,8,1]{2,1,0:T(8,128)S(1)}, u32[]{:S(2)}, u32[]{:S(2)}) collective-permute-start(f32[4,8,1]{2,1,0:T(8,128)S(1)} %get-tuple-element.140), channel_id=1, source_target_pairs={{1,0},{2,1},{3,2},{4,3},{5,4},{6,5},{7,6},{9,8},{10,9},{11,10},{12... | collective-permute-start | bytes 392 | tf_op jit(solution)/shard_map/ppermute | solution.py:22
  246.6 8.5 %collective-permute-start.17 = (f32[4,8,1]{2,1,0:T(8,128)S(1)}, f32[4,8,1]{2,1,0:T(8,128)S(1)}, u32[]{:S(2)}, u32[]{:S(2)}) collective-permute-start(f32[4,8,1]{2,1,0:T(8,128)S(1)} %get-tuple-element.135), channel_id=1, source_target_pairs={{0,1},{1,2},{2,3},{3,4},{4,5},{5,6},{6,7},{8,9},{9,10},{10,11},{11... | collective-permute-start | bytes 392 | tf_op jit(solution)/shard_map/ppermute | solution.py:21
  248.5 13.1 %collective-permute-start.15 = (f32[4,1,128]{2,1,0:T(1,128)S(1)}, f32[4,1,128]{2,1,0:T(1,128)S(1)}, u32[]{:S(2)}, u32[]{:S(2)}) collective-permute-start(f32[4,1,128]{2,1,0:T(1,128)S(1)} %get-tuple-element.133), channel_id=1, source_target_pairs={{0,8},{8,16},{16,24},{1,9},{9,17},{17,25},{2,10},{10,18},{18,26},{... | collective-permute-start | bytes 6152 | tf_op jit(solution)/shard_map/ppermute | solution.py:21
  250.9 10.8 %collective-permute-start.14 = (f32[4,1,128]{2,1,0:T(1,128)S(1)}, f32[4,1,128]{2,1,0:T(1,128)S(1)}, u32[]{:S(2)}, u32[]{:S(2)}) collective-permute-start(f32[4,1,128]{2,1,0:T(1,128)S(1)} %get-tuple-element.132), channel_id=1, source_target_pairs={{8,0},{16,8},{24,16},{9,1},{17,9},{25,17},{10,2},{18,10},{26,18},{... | collective-permute-start | bytes 6152 | tf_op jit(solution)/shard_map/ppermute | solution.py:22
  252.2 9.5 %collective-permute-start.13 = (f32[1,8,128]{2,1,0:T(8,128)S(1)}, f32[1,8,128]{2,1,0:T(8,128)S(1)}, u32[]{:S(2)}, u32[]{:S(2)}) collective-permute-start(f32[1,8,128]{2,1,0:T(8,128)S(1)} %get-tuple-element.131), channel_id=1, source_target_pairs={{0,32},{32,64},{64,96},{96,128},{128,160},{160,192},{192,224},{224... | collective-permute-start | bytes 12296 | tf_op jit(solution)/shard_map/ppermute | solution.py:21
  253.5 8.2 %collective-permute-start.12 = (f32[1,8,128]{2,1,0:T(8,128)S(1)}, f32[1,8,128]{2,1,0:T(8,128)S(1)}, u32[]{:S(2)}, u32[]{:S(2)}) collective-permute-start(f32[1,8,128]{2,1,0:T(8,128)S(1)} %get-tuple-element.130), channel_id=1, source_target_pairs={{32,0},{64,32},{96,64},{128,96},{160,128},{192,160},{224,192},{256... | collective-permute-start | bytes 12296 | tf_op jit(solution)/shard_map/ppermute | solution.py:22
  255.1 6.6 %collective-permute-start.16 = (f32[4,8,1]{2,1,0:T(8,128)S(1)}, f32[4,8,1]{2,1,0:T(8,128)S(1)}, u32[]{:S(2)}, u32[]{:S(2)}) collective-permute-start(f32[4,8,1]{2,1,0:T(8,128)S(1)} %get-tuple-element.134), channel_id=1, source_target_pairs={{1,0},{2,1},{3,2},{4,3},{5,4},{6,5},{7,6},{9,8},{10,9},{11,10},{12... | collective-permute-start | bytes 392 | tf_op jit(solution)/shard_map/ppermute | solution.py:22
